TPU v7x, 32 devices: a whole 2x2x4 slice. The times are simulated.
32 devices in a mesh: dev: 16 (over z, y, x), rep: 2 (over core).
Axes of the slice: x: 2, y: 2, z: 4, core: 2. Of those that a mesh axis runs over, the one named last changes fastest.
Arguments:
- node_features: bfloat16 [1024, 2, 3136], P('dev', 'rep'), may hold values from -6 to 6
- src_node: int32 [16, 16, 2], P('dev'), may hold values from 0 to 63
- dst_node: int32 [16, 16, 2], P('dev'), may hold values from 0 to 63
- counts: int32 [16, 16], P('dev'), may hold values from 1 to 2, as said below
- rotation: bfloat16 [16, 16, 2, 235], P('dev'), may hold values from -2 to 2
- w_zero: bfloat16 [896, 2, 448], P(None, 'rep'), may hold values from -0.1875 to 0.1875
- w_one: bfloat16 [2, 768, 2, 384], P(None, None, 'rep'), may hold values from -0.15625 to 0.15625
- w_two: bfloat16 [2, 640, 2, 320], P(None, None, 'rep'), may hold values from -0.15625 to 0.15625
- norm_gain: float32 [2, 3136], P('rep'), may hold values from 0.5 to 1.5
Outputs:
- updated: bfloat16 [1024, 2, 3136], P('dev', 'rep')
Inputs may be any that keep to these rules, and one draw needn't show every extreme that they name: Slots i < counts[s, d] hold edges, the others padding; in every draw some destination device receives 2 edges from every source device.
All inputs are finite; a program needn't handle non-finite values.
Results may differ from a plain program's by a relative error of at most 0.0054.
Values may be sent and summed in bfloat16 or wider, within the bound.
A program may use at most 64 MiB of HBM per device.

v0:
```python
import functools

import jax
import jax.numpy as jnp
from jax import lax
from jax.experimental import pallas as pl
from jax.experimental.pallas import tpu as pltpu
from jax.sharding import PartitionSpec as P

LANES = 128
HALF = 64
COEFFS = 49
FRAME = 29
ROT = 235
WINDOW = 120
TILES = (COEFFS + 1) // 2
WIDE = TILES * LANES
MESSAGE = (FRAME + 1) // 2 * LANES
VMEM_LIMIT = 40 * 1024 * 1024
BLOCK = 32
MESH = pl.DeviceIdType.MESH


def frame_slot(degree, order):
    if order == 0:
        return degree
    if order == 1:
        return 6 + degree
    if order == -1:
        return 12 + degree
    if order == 2:
        return 17 + degree
    return 22 + degree


def terms():
    listing = []
    spot = 0
    for degree in range(7):
        reach = min(degree, 2)
        span = 2 * degree + 1
        first = degree * degree
        for row in range(2 * reach + 1):
            slot = frame_slot(degree, row - reach)
            for tile in range(first // 2, (first + span - 1) // 2 + 1):
                ends = []
                for coeff in (2 * tile, 2 * tile + 1):
                    inside = first <= coeff < first + span
                    ends.append(spot + row * span + coeff - first if inside else None)
                listing.append((slot, tile, ends[0], ends[1]))
        spot += span * (2 * reach + 1)
    return listing


TERMS = terms()


def message_place(slot):
    return slot // 2, slot % 2


def far_first(count):
    return sorted(range(1, count), key=lambda offset: -min(offset, count - offset))


def each_peer(count, func):
    if count <= 17:
        for offset in far_first(count):
            func(offset - 1)
    else:
        each(count - 1, func)


def each(count, func):
    if count <= 16:
        for index in range(count):
            func(index)
    else:
        lax.fori_loop(0, count, lambda index, carry: (func(index), carry)[1], 0)


def kernel(
    peers,
    slots,
    x_hbm,
    rot_hbm,
    src_hbm,
    cnt_hbm,
    dst_hbm,
    gain_hbm,
    w0_hbm,
    w1_hbm,
    w2_hbm,
    out_ref,
    x_ref,
    rot_ref,
    src_ref,
    cnt_ref,
    dst_ref,
    gain_ref,
    w0,
    w1,
    w2,
    low_scr,
    high_scr,
    xg,
    own,
    packed,
    other,
    lhs,
    y_scr,
    msg,
    recv,
    rrot,
    mult,
    f_scr,
    back,
    total,
    sq,
    sq_other,
    wsem,
    esem,
    rot_send,
    rot_recv,
    msg_send,
    msg_recv,
    qsem,
):
    me = lax.axis_index("dev")
    half = lax.axis_index("rep")
    nodes = x_ref.shape[0]
    flat = x_ref.shape[1]
    blocks = peers * slots // BLOCK
    group = BLOCK // slots
    partner = {"rep": 1 - half}

    def peer(offset):
        return lax.rem(me + offset, peers)

    loads = [
        pltpu.make_async_copy(src, dst, wsem.at[index])
        for index, (src, dst) in enumerate(
            (
                (x_hbm, x_ref),
                (rot_hbm, rot_ref),
                (src_hbm, src_ref),
                (cnt_hbm, cnt_ref),
                (dst_hbm, dst_ref),
                (gain_hbm, gain_ref),
                (w0_hbm, w0),
                (w1_hbm, w1),
                (w2_hbm, w2),
            )
        )
    ]
    for copy in loads:
        copy.start()
    barrier = pltpu.get_barrier_semaphore()
    pl.semaphore_signal(barrier, inc=1, device_id=partner, device_id_type=MESH)
    each(
        peers - 1,
        lambda o: pl.semaphore_signal(
            barrier, inc=1, device_id={"dev": peer(o + 1)}, device_id_type=MESH
        ),
    )

    lane = lax.broadcasted_iota(jnp.int32, (BLOCK, LANES), 1)
    low_half = lane < HALF
    mine = (lane // HALF) == half

    y_scr[...] = jnp.zeros_like(y_scr)
    xg[:, (TILES - 1) * LANES :] = jnp.zeros((BLOCK, LANES), jnp.float32)
    low_scr[...] = jnp.zeros_like(low_scr)
    high_scr[...] = jnp.zeros_like(high_scr)

    def column(rows):
        row = lax.broadcasted_iota(jnp.int32, (BLOCK, group), 0)
        spot = lax.broadcasted_iota(jnp.int32, (BLOCK, group), 1)
        chosen = jnp.zeros((BLOCK, group), jnp.float32)
        for index in range(slots):
            chosen = jnp.where(row == spot * slots + index, rows[index], chosen)
        return jnp.sum(chosen, axis=1, keepdims=True)

    def sources(block):
        count = cnt_ref[block]
        value = src_ref[block]
        return column(
            [
                jnp.where(count > index, value[index : index + 1], -1).astype(jnp.float32)
                for index in range(slots)
            ]
        )

    def targets(block):
        value = dst_ref[block].astype(jnp.float32)
        down = column([value[index : index + 1] for index in range(slots)])
        row = lax.broadcasted_iota(jnp.int32, (BLOCK, BLOCK), 0)
        spot = lax.broadcasted_iota(jnp.int32, (BLOCK, BLOCK), 1)
        return jnp.sum(jnp.where(row == spot, down, 0.0), axis=0, keepdims=True)

    def load_rotation(ref, start):
        for index in range(group):
            rows = ref[start + index].astype(jnp.float32)
            low_scr[index * slots : (index + 1) * slots, 0:WINDOW] = rows[:, 0:WINDOW]
            high_scr[index * slots : (index + 1) * slots, 0:WINDOW] = rows[:, ROT - WINDOW :]
        return low_scr[...], high_scr[...]

    def multiplier(tables, first, second):
        given = [entry for entry in (first, second) if entry is not None]
        which = 0 if max(given) < WINDOW else 1
        shift = which * (ROT - WINDOW)
        places = [WINDOW if e is None else e - shift for e in (first, second)]
        index = jnp.where(low_half, places[0], places[1])
        return jnp.take_along_axis(tables[which], index, axis=1, mode="promise_in_bounds")

    def turn(block):
        tables = load_rotation(rot_ref, block * group)
        hot = (
            lax.broadcasted_iota(jnp.int32, (BLOCK, nodes), 1).astype(jnp.float32) == sources(block)
        ).astype(jnp.bfloat16)
        xg[:, 0:flat] = jnp.dot(hot, x_ref[...], preferred_element_type=jnp.float32)
        sums = [None] * FRAME
        for slot, tile, first, second in TERMS:
            part = multiplier(tables, first, second) * xg[:, tile * LANES : (tile + 1) * LANES]
            sums[slot] = part if sums[slot] is None else sums[slot] + part
        for slot in range(FRAME):
            sums[slot] = sums[slot] + pltpu.roll(sums[slot], HALF, 1)
            own[block, :, slot * LANES : (slot + 1) * LANES] = sums[slot]
        for pair in range((FRAME + 1) // 2):
            first = sums[2 * pair]
            second = sums[min(2 * pair + 1, FRAME - 1)]
            packed[block, :, pair * LANES : (pair + 1) * LANES] = jnp.where(
                mine, first, second
            ).astype(jnp.bfloat16)

    for copy in loads[:4]:
        copy.wait()
    each(blocks, turn)

    pl.semaphore_wait(barrier, peers)

    exchange = pltpu.make_async_remote_copy(
        src_ref=packed,
        dst_ref=other,
        send_sem=esem.at[0],
        recv_sem=esem.at[1],
        device_id=partner,
        device_id_type=MESH,
    )
    exchange.start()

    def transfer(source, target, send, receive, o, landing):
        to = peer(o + 1)
        spot = me if landing is None else landing
        return pltpu.make_async_remote_copy(
            src_ref=source.at[to],
            dst_ref=target.at[spot],
            send_sem=send.at[to],
            recv_sem=receive.at[spot],
            device_id={"dev": to},
            device_id_type=MESH,
        )

    def rotations(o, landing=None):
        return transfer(rot_ref, rrot, rot_send, rot_recv, o, landing)

    def messages(o, landing=None):
        return transfer(msg, recv, msg_send, msg_recv, o, landing)

    each_peer(peers, lambda o: rotations(o).start())
    rrot[me] = rot_ref[me]

    for copy in loads[4:]:
        copy.wait()
    exchange.wait()

    def mix(block):
        for pair in range((FRAME + 1) // 2):
            there = other[block, :, pair * LANES : (pair + 1) * LANES].astype(jnp.float32)
            for slot, value in ((2 * pair, there), (2 * pair + 1, None)):
                if slot < FRAME:
                    value = pltpu.roll(there, HALF, 1) if value is None else value
                    cols = slice(slot * LANES, (slot + 1) * LANES)
                    lhs[:, cols] = jnp.where(mine, own[block, :, cols], value).astype(jnp.bfloat16)
        nt = (((1,), (1,)), ((), ()))
        y_scr[:, 0 : 7 * HALF] = lax.dot_general(
            lhs[:, 0 : 7 * LANES], w0[...], nt, preferred_element_type=jnp.float32
        )
        for start, count, ref, dims in (
            (7, 6, w1, (((1,), (0,)), ((), ()))),
            (19, 5, w2, nt),
        ):
            rows = jnp.concatenate(
                [
                    lhs[:, start * LANES : (start + count) * LANES],
                    lhs[:, (start + count) * LANES : (start + 2 * count) * LANES],
                ],
                axis=0,
            )
            real = lax.dot_general(rows, ref[0], dims, preferred_element_type=jnp.float32)
            imag = lax.dot_general(rows, ref[1], dims, preferred_element_type=jnp.float32)
            width = count * HALF
            plus = start * HALF
            minus = plus + width
            y_scr[:, plus : plus + width] = real[:BLOCK] - imag[BLOCK:]
            y_scr[:, minus : minus + width] = imag[:BLOCK] + real[BLOCK:]
        for index in range(group):
            msg[block * group + index] = y_scr[index * slots : (index + 1) * slots, :].astype(
                jnp.bfloat16
            )

    each(blocks, mix)
    each_peer(peers, lambda o: messages(o).start())
    recv[me] = msg[me]

    def wait_rotation(o):
        rotations(o, peer(o + 1)).wait_recv()

    def wait_message(o):
        messages(o, peer(o + 1)).wait_recv()

    each(peers - 1, wait_rotation)

    def prepare(block):
        tables = load_rotation(rrot, block * group)
        for number, (slot, tile, first, second) in enumerate(TERMS):
            mult[number] = multiplier(tables, first, second)

    def collect(block, add):
        for index in range(group):
            f_scr[index * slots : (index + 1) * slots, :] = recv[block * group + index].astype(
                jnp.float32
            )
        doubled = {}
        for slot in range(FRAME):
            tile, side = message_place(slot)
            value = f_scr[:, tile * LANES : (tile + 1) * LANES]
            turned = pltpu.roll(value, HALF, 1)
            doubled[slot] = (
                jnp.where(low_half, value, turned) if side == 0 else jnp.where(low_half, turned, value)
            )
        sums = [None] * TILES
        for number, (slot, tile, first, second) in enumerate(TERMS):
            part = mult[number] * doubled[slot]
            sums[tile] = part if sums[tile] is None else sums[tile] + part
        for tile in range(TILES):
            back[:, tile * LANES : (tile + 1) * LANES] = sums[tile].astype(jnp.bfloat16)
        hot = (
            lax.broadcasted_iota(jnp.int32, (nodes, BLOCK), 0).astype(jnp.float32) == targets(block)
        ).astype(jnp.bfloat16)
        value = jnp.dot(hot, back[...], preferred_element_type=jnp.float32)
        total[...] = total[...] + value if add else value

    if blocks == 1:
        prepare(0)
        each(peers - 1, wait_message)
        collect(0, False)
    else:
        each(peers - 1, wait_message)
        total[...] = jnp.zeros_like(total)

        def one(block, carry):
            prepare(block)
            collect(block, True)
            return carry

        lax.fori_loop(0, blocks, one, 0)

    partial = None
    for tile in range(TILES):
        value = total[:, tile * LANES : (tile + 1) * LANES]
        partial = value * value if partial is None else partial + value * value
    sq[...] = partial
    share = pltpu.make_async_remote_copy(
        src_ref=sq,
        dst_ref=sq_other,
        send_sem=qsem.at[0],
        recv_sem=qsem.at[1],
        device_id=partner,
        device_id_type=MESH,
    )
    share.start()
    each(peers - 1, lambda o: rotations(o).wait_send())
    each(peers - 1, lambda o: messages(o).wait_send())
    share.wait()
    mean_sq = jnp.sum(sq[...] + sq_other[...], axis=1, keepdims=True) / (2 * flat)
    scale = lax.rsqrt(mean_sq + 1e-06)
    for start in range(0, flat, LANES):
        cols = slice(start, min(start + LANES, flat))
        normed = total[:, cols] * scale
        out_ref[:, cols] = (
            x_ref[:, cols].astype(jnp.float32) + gain_ref[:, cols] * normed
        ).astype(jnp.bfloat16)


def shards(node_features, src_node, dst_node, counts, rotation, w_zero, w_one, w_two, norm_gain):
    nodes, _, flat = node_features.shape
    peers, slots = src_node.shape[1:]
    edges = peers * slots
    blocks = edges // BLOCK
    x = node_features.reshape(nodes, flat)
    group = peers // blocks
    src = src_node.reshape(blocks, group, slots).swapaxes(1, 2)
    dst = dst_node.reshape(blocks, group, slots).swapaxes(1, 2)
    cnt = counts.reshape(blocks, 1, group)
    rot = rotation.reshape(peers, slots, ROT)
    w0 = w_zero.reshape(w_zero.shape[0], -1).T
    w1 = w_one.reshape(2, w_one.shape[1], -1)
    w2 = w_two.reshape(2, w_two.shape[1], -1).swapaxes(1, 2)
    vmem = pl.BlockSpec(memory_space=pltpu.VMEM)
    hbm = pl.BlockSpec(memory_space=pltpu.HBM)
    f32, bf16 = jnp.float32, jnp.bfloat16
    dma = pltpu.SemaphoreType.DMA
    pairs = (FRAME + 1) // 2
    operands = (x, rot, src, cnt, dst, norm_gain, w0, w1, w2)
    out = pl.pallas_call(
        functools.partial(kernel, peers, slots),
        out_shape=jax.ShapeDtypeStruct((nodes, flat), bf16),
        in_specs=[hbm] * 9,
        out_specs=vmem,
        scratch_shapes=[
            pltpu.VMEM(x.shape, bf16),
            pltpu.VMEM(rot.shape, bf16),
            pltpu.VMEM(src.shape, jnp.int32),
            pltpu.VMEM(cnt.shape, jnp.int32),
            pltpu.VMEM(dst.shape, jnp.int32),
            pltpu.VMEM(norm_gain.shape, f32),
            pltpu.VMEM(w0.shape, bf16),
            pltpu.VMEM(w1.shape, bf16),
            pltpu.VMEM(w2.shape, bf16),
            pltpu.VMEM((BLOCK, LANES), f32),
            pltpu.VMEM((BLOCK, LANES), f32),
            pltpu.VMEM((BLOCK, WIDE), f32),
            pltpu.VMEM((blocks, BLOCK, FRAME * LANES), f32),
            pltpu.VMEM((blocks, BLOCK, pairs * LANES), bf16),
            pltpu.VMEM((blocks, BLOCK, pairs * LANES), bf16),
            pltpu.VMEM((BLOCK, FRAME * LANES), bf16),
            pltpu.VMEM((BLOCK, MESSAGE), f32),
            pltpu.VMEM((peers, slots, MESSAGE), bf16),
            pltpu.VMEM((peers, slots, MESSAGE), bf16),
            pltpu.VMEM((peers, slots, ROT), bf16),
            pltpu.VMEM((len(TERMS), BLOCK, LANES), f32),
            pltpu.VMEM((BLOCK, MESSAGE), f32),
            pltpu.VMEM((BLOCK, WIDE), bf16),
            pltpu.VMEM((nodes, WIDE), f32),
            pltpu.VMEM((nodes, LANES), f32),
            pltpu.VMEM((nodes, LANES), f32),
            dma((9,)),
            dma((2,)),
            dma((peers,)),
            dma((peers,)),
            dma((peers,)),
            dma((peers,)),
            dma((2,)),
        ],
        compiler_params=pltpu.CompilerParams(
            collective_id=0, has_side_effects=True, vmem_limit_bytes=VMEM_LIMIT
        ),
    )(*(pltpu.with_memory_space_constraint(operand, pltpu.HBM) for operand in operands))
    return out.reshape(nodes, 1, flat)


def solution(mesh):
    return jax.shard_map(
        shards,
        mesh=mesh,
        in_specs=(
            P("dev", "rep", None),
            P("dev", None, None),
            P("dev", None, None),
            P("dev", None),
            P("dev", None, None, None),
            P(None, "rep", None),
            P(None, None, "rep", None),
            P(None, None, "rep", None),
            P("rep", None),
        ),
        out_specs=P("dev", "rep", None),
        check_vma=False,
    )
```

profile of v0, /device:TPU:0, one launch (start us, length us, event | category | flops | bytes accessed | tf_op | source)
XLA Modules:
  0.0 17.4 jit_solution(2897565618643018449)
XLA Ops:
  0.0 16.6 %shard_map.91 = bf16[64,3136]{1,0:T(8,128)(2,1)S(1)} custom-call(bf16[64,3136]{1,0:T(8,128)(2,1)} %bitcast.17, bf16[16,2,235]{2,1,0:T(2,128)(2,1)} %bitcast.18, s32[1,2,16]{2,1,0:T(2,128)} %bitcast.19, s32[1,1,16]{2,1,0:T(1,128)} %bitcast.21, s32[1,2,16]{2,1,0:T(2,128)} %bitcast.20, f32[1,3136]{1,0:T(1,128)} %gain_hbm.1, bf16[448,896]{1,0:T(8,128)(2,1)} %bitcast.16, ...), custom_call_target="tpu_custom_call" | custom-call | tf_op jit(solution)/shard_map/pallas_call | solution.py:416
  16.6 0.8 %copy.11 = bf16[64,1,3136]{2,0,1:T(8,128)(2,1)} copy(bf16[64,1,3136]{2,0,1:T(8,128)(2,1)S(1)} %bitcast.13) | data formatting | bytes 802816
where the time goes:
time: 17.5 us; the launch traced here: 17.4 us
  Pallas kernels  16.6 us (95%)
  local copies, waits for them, and re-layouts  0.75 us (4%)
    pallas_call x1, Pallas kernels, shards(): pl.pallas_call(functools.partial(kernel, peers, slots), out_shape=jax.Sha...  16.6 us
    unnamed x1, local copies, waits for them, and re-layouts  0.75 us

commit v1 on v0

--- a/solution.py
+++ b/solution.py
@@ -120,10 +120,8 @@
     sq_other,
     wsem,
     esem,
-    rot_send,
-    rot_recv,
-    msg_send,
-    msg_recv,
+    rot_sem,
+    msg_sem,
     qsem,
 ):
     me = lax.axis_index("dev")
@@ -249,23 +247,35 @@
     )
     exchange.start()
 
-    def transfer(source, target, send, receive, o, landing):
+    def transfer(source, target, send, receive, o):
         to = peer(o + 1)
-        spot = me if landing is None else landing
         return pltpu.make_async_remote_copy(
             src_ref=source.at[to],
-            dst_ref=target.at[spot],
-            send_sem=send.at[to],
-            recv_sem=receive.at[spot],
+            dst_ref=target.at[me],
+            send_sem=send,
+            recv_sem=receive,
             device_id={"dev": to},
             device_id_type=MESH,
         )
 
-    def rotations(o, landing=None):
-        return transfer(rot_ref, rrot, rot_send, rot_recv, o, landing)
-
-    def messages(o, landing=None):
-        return transfer(msg, recv, msg_send, msg_recv, o, landing)
+    def rotations(o):
+        return transfer(rot_ref, rrot, rot_sem.at[0], rot_sem.at[1], o)
+
+    def messages(o):
+        return transfer(msg, recv, msg_sem.at[0], msg_sem.at[1], o)
+
+    def everything(source, target, sems):
+        return pltpu.make_async_remote_copy(
+            src_ref=source.at[pl.ds(0, peers - 1)],
+            dst_ref=target.at[pl.ds(0, peers - 1)],
+            send_sem=sems.at[0],
+            recv_sem=sems.at[1],
+            device_id={"dev": peer(1)},
+            device_id_type=MESH,
+        )
+
+    all_rotations = everything(rot_ref, rrot, rot_sem)
+    all_messages = everything(msg, recv, msg_sem)
 
     each_peer(peers, lambda o: rotations(o).start())
     rrot[me] = rot_ref[me]
@@ -313,13 +323,7 @@
     each_peer(peers, lambda o: messages(o).start())
     recv[me] = msg[me]
 
-    def wait_rotation(o):
-        rotations(o, peer(o + 1)).wait_recv()
-
-    def wait_message(o):
-        messages(o, peer(o + 1)).wait_recv()
-
-    each(peers - 1, wait_rotation)
+    all_rotations.wait_recv()
 
     def prepare(block):
         tables = load_rotation(rrot, block * group)
@@ -353,10 +357,10 @@
 
     if blocks == 1:
         prepare(0)
-        each(peers - 1, wait_message)
+        all_messages.wait_recv()
         collect(0, False)
     else:
-        each(peers - 1, wait_message)
+        all_messages.wait_recv()
         total[...] = jnp.zeros_like(total)
 
         def one(block, carry):
@@ -380,8 +384,8 @@
         device_id_type=MESH,
     )
     share.start()
-    each(peers - 1, lambda o: rotations(o).wait_send())
-    each(peers - 1, lambda o: messages(o).wait_send())
+    all_rotations.wait_send()
+    all_messages.wait_send()
     share.wait()
     mean_sq = jnp.sum(sq[...] + sq_other[...], axis=1, keepdims=True) / (2 * flat)
     scale = lax.rsqrt(mean_sq + 1e-06)
@@ -447,10 +451,8 @@
             pltpu.VMEM((nodes, LANES), f32),
             dma((9,)),
             dma((2,)),
-            dma((peers,)),
-            dma((peers,)),
-            dma((peers,)),
-            dma((peers,)),
+            dma((2,)),
+            dma((2,)),
             dma((2,)),
         ],
         compiler_params=pltpu.CompilerParams(

time: 17.5 us -> 17 us (0.971)
  Pallas kernels: 16.6 us -> 16.1 us
    pallas_call x1, Pallas kernels: 16.6 us -> 16.1 us  [shards(): pl.pallas_call(functools.partial(kernel, peers, slots), out_shape=jax.Sha...]
where the time goes in v1:
time: 17 us; the launch traced here: 16.9 us
  Pallas kernels  16.1 us (95%)
  local copies, waits for them, and re-layouts  0.75 us (4%)
    pallas_call x1, Pallas kernels, shards(): pl.pallas_call(functools.partial(kernel, peers, slots), out_shape=jax.Sha...  16.1 us
    unnamed x1, local copies, waits for them, and re-layouts  0.75 us

profile of v1, /device:TPU:0, one launch (start us, length us, event | category | flops | bytes accessed | tf_op | source)
XLA Modules:
  0.0 16.9 jit_solution(13483833896201206629)
XLA Ops:
  0.0 16.1 %shard_map.91 = bf16[64,3136]{1,0:T(8,128)(2,1)S(1)} custom-call(bf16[64,3136]{1,0:T(8,128)(2,1)} %bitcast.17, bf16[16,2,235]{2,1,0:T(2,128)(2,1)} %bitcast.18, s32[1,2,16]{2,1,0:T(2,128)} %bitcast.19, s32[1,1,16]{2,1,0:T(1,128)} %bitcast.21, s32[1,2,16]{2,1,0:T(2,128)} %bitcast.20, f32[1,3136]{1,0:T(1,128)} %gain_hbm.1, bf16[448,896]{1,0:T(8,128)(2,1)} %bitcast.16, ...), custom_call_target="tpu_custom_call" | custom-call | tf_op jit(solution)/shard_map/pallas_call | solution.py:420
  16.1 0.8 %copy.11 = bf16[64,1,3136]{2,0,1:T(8,128)(2,1)} copy(bf16[64,1,3136]{2,0,1:T(8,128)(2,1)S(1)} %bitcast.13) | data formatting | bytes 802816

commit v2 on v1

v2 whole, which is shorter than its diff:
```python
import functools

import jax
import jax.numpy as jnp
from jax import lax
from jax.experimental import pallas as pl
from jax.experimental.pallas import tpu as pltpu
from jax.sharding import PartitionSpec as P

LANES = 128
HALF = 64
COEFFS = 49
FRAME = 29
ROT = 235
TILES = (COEFFS + 1) // 2
WIDE = TILES * LANES
MESSAGE = (FRAME + 1) // 2 * LANES
VMEM_LIMIT = 40 * 1024 * 1024
BLOCK = 32
MESH = pl.DeviceIdType.MESH
ORDERS = ((0, 7), (7, 6), (13, 6), (19, 5), (24, 5))
SEND_ORDER = (0, 4, 1, 2, 3)


def frame_slot(degree, order):
    if order == 0:
        return degree
    if order == 1:
        return 6 + degree
    if order == -1:
        return 12 + degree
    if order == 2:
        return 17 + degree
    return 22 + degree


def listings():
    groups = []
    parts = []
    segments = []
    spot = 0
    for degree in range(7):
        reach = min(degree, 2)
        span = 2 * degree + 1
        first = degree * degree
        for row in range(2 * reach + 1):
            slot = frame_slot(degree, row - reach)
            base = spot + row * span - first
            segments.append((base + first, (-base) % 4))
            for quad in range(first // 4, (first + span - 1) // 4 + 1):
                low = base + max(4 * quad, first)
                high = base + min(4 * quad + 3, first + span - 1)
                for window in (0, 1):
                    start = max(low, window * LANES)
                    end = min(high, window * LANES + LANES - 1)
                    if start <= end:
                        for which in (0, 1):
                            tile = 2 * quad + which
                            if any((e - base) // 2 == tile for e in range(start, end + 1)):
                                parts.append((slot, tile, len(groups), which))
                        groups.append((window, start, end))
        spot += span * (2 * reach + 1)
    return groups, parts, segments


GROUPS, PARTS, SEGMENTS = listings()
LOW_ROWS = BLOCK * sum(window == 0 for window, _, _ in GROUPS)
ALL_ROWS = BLOCK * len(GROUPS)


def packed_pairs():
    pairs = []
    starts = []
    for first, count in ORDERS:
        starts.append(len(pairs) * LANES)
        for slot in range(first, first + count, 2):
            pairs.append((slot, min(slot + 1, first + count - 1)))
    return pairs, starts


PAIRS, STARTS = packed_pairs()


def message_starts():
    starts = {}
    spot = 0
    for order in SEND_ORDER:
        starts[order] = spot
        spot += ORDERS[order][1] * HALF
    return starts


SENT = message_starts()
SPLIT = (ORDERS[3][1] + 1) // 2 * LANES


def message_place(slot):
    order = max(o for o, (first, _) in enumerate(ORDERS) if first <= slot)
    place = SENT[order] // HALF + slot - ORDERS[order][0]
    return place // 2, place % 2


def far_first(count):
    return sorted(range(1, count), key=lambda offset: -min(offset, count - offset))


def each_peer(count, func):
    if count <= 17:
        for offset in far_first(count):
            func(offset - 1)
    else:
        each(count - 1, func)


def each(count, func):
    if count <= 16:
        for index in range(count):
            func(index)
    else:
        lax.fori_loop(0, count, lambda index, carry: (func(index), carry)[1], 0)


def kernel(
    peers,
    slots,
    x_hbm,
    rot_hbm,
    src_hbm,
    cnt_hbm,
    dst_hbm,
    w0_hbm,
    w1_hbm,
    w2_hbm,
    x_ref,
    total,
    sums_ref,
    rot_ref,
    src_ref,
    cnt_ref,
    dst_ref,
    w0_raw,
    w2_raw,
    w0,
    w1,
    w2,
    expand,
    rot_scr,
    entries,
    mult,
    xg,
    turned,
    part_scr,
    y_scr,
    msg,
    recv,
    rrot,
    f_scr,
    back,
    sq,
    sq_other,
    wsem,
    esem,
    rot_sem,
    msg_sem,
    qsem,
):
    me = lax.axis_index("dev")
    half = lax.axis_index("rep")
    nodes = x_ref.shape[0]
    flat = x_ref.shape[1]
    blocks = peers * slots // BLOCK
    group = BLOCK // slots
    partner = {"rep": 1 - half}

    def peer(offset):
        return lax.rem(me + offset, peers)

    def load(index, src, dst):
        return pltpu.make_async_copy(src, dst, wsem.at[index])

    early = [
        load(0, rot_hbm, rot_ref),
        load(1, src_hbm, src_ref),
        load(2, cnt_hbm, cnt_ref),
        load(3, x_hbm, x_ref),
    ]
    late = [load(4, dst_hbm, dst_ref), load(5, w0_hbm, w0_raw), load(6, w2_hbm, w2_raw)]
    width = w1_hbm.shape[-1]
    for side in (0, 1):
        for kind in (0, 1):
            cols = slice(kind * width, (kind + 1) * width)
            late.append(load(7, w1_hbm.at[kind, :, side], w1.at[side, :, :, cols]))
    waits = late[:3] + [load(7, w1, w1)]
    for copy in early + late:
        copy.start()
    barrier = pltpu.get_barrier_semaphore()
    pl.semaphore_signal(barrier, inc=1, device_id=partner, device_id_type=MESH)
    each(
        peers - 1,
        lambda o: pl.semaphore_signal(
            barrier, inc=1, device_id={"dev": peer(o + 1)}, device_id_type=MESH
        ),
    )

    lane = lax.broadcasted_iota(jnp.int32, (BLOCK, LANES), 1)
    low_half = lane < HALF

    y_scr[...] = jnp.zeros_like(y_scr)
    xg[:, flat:] = jnp.zeros((BLOCK, xg.shape[1] - flat), jnp.float32)
    for window in (0, 1):
        entry = lax.broadcasted_iota(jnp.int32, (LANES, LANES), 0) + window * LANES
        spot = lax.broadcasted_iota(jnp.int32, (LANES, LANES), 1)
        shift = jnp.zeros_like(entry)
        for start, offset in SEGMENTS:
            shift = jnp.where(entry >= start, offset, shift)
        place = lax.rem(entry + shift, 4)
        for side in (0, 1):
            hit = place == lax.div(spot, HALF) + 2 * side
            expand[window, :, side * LANES : (side + 1) * LANES] = jnp.where(
                hit, 1.0, 0.0
            ).astype(jnp.bfloat16)

    def column(rows):
        row = lax.broadcasted_iota(jnp.int32, (BLOCK, group), 0)
        spot = lax.broadcasted_iota(jnp.int32, (BLOCK, group), 1)
        chosen = jnp.zeros((BLOCK, group), jnp.float32)
        for index in range(slots):
            chosen = jnp.where(row == spot * slots + index, rows[index], chosen)
        return jnp.sum(chosen, axis=1, keepdims=True)

    def sources(block):
        count = cnt_ref[block]
        value = src_ref[block]
        return column(
            [
                jnp.where(count > index, value[index : index + 1], -1).astype(jnp.float32)
                for index in range(slots)
            ]
        )

    def targets(block):
        value = dst_ref[block].astype(jnp.float32)
        down = column([value[index : index + 1] for index in range(slots)])
        row = lax.broadcasted_iota(jnp.int32, (BLOCK, BLOCK), 0)
        spot = lax.broadcasted_iota(jnp.int32, (BLOCK, BLOCK), 1)
        return jnp.sum(jnp.where(row == spot, down, 0.0), axis=0, keepdims=True)

    def spread(ref, start):
        for index in range(group):
            rot_scr[index * slots : (index + 1) * slots, 0:ROT] = ref[start + index].astype(
                jnp.float32
            )
        for number, (window, first, last) in enumerate(GROUPS):
            spots = lane + window * LANES
            rows = rot_scr[:, window * LANES : (window + 1) * LANES]
            entries[number * BLOCK : (number + 1) * BLOCK, :] = jnp.where(
                (spots >= first) & (spots <= last), rows, 0.0
            ).astype(jnp.bfloat16)
        for window, rows in enumerate((slice(0, LOW_ROWS), slice(LOW_ROWS, ALL_ROWS))):
            mult[rows] = jnp.dot(
                entries[rows], expand[window], preferred_element_type=jnp.float32
            )

    def factor(number, which):
        return mult[number * BLOCK : (number + 1) * BLOCK, which * LANES : (which + 1) * LANES]

    def turn(block):
        spread(rot_ref, block * group)
        if block is first_block:
            for copy in early[1:]:
                copy.wait()
        hot = (
            lax.broadcasted_iota(jnp.int32, (BLOCK, nodes), 1).astype(jnp.float32) == sources(block)
        ).astype(jnp.bfloat16)
        xg[:, 0:flat] = jnp.dot(hot, x_ref[...], preferred_element_type=jnp.float32)
        sums = [None] * FRAME
        for slot, tile, number, which in PARTS:
            part = factor(number, which) * xg[:, tile * LANES : (tile + 1) * LANES]
            sums[slot] = part if sums[slot] is None else sums[slot] + part
        for pair, (one, two) in enumerate(PAIRS):
            kept = jnp.where(low_half, sums[one], sums[two])
            moved = jnp.where(low_half, sums[two], sums[one])
            turned[half, block, :, pair * LANES : (pair + 1) * LANES] = (
                kept + pltpu.roll(moved, HALF, 1)
            ).astype(jnp.bfloat16)

    early[0].wait()
    first_block = 0 if blocks <= 16 else None
    if first_block is None:
        for copy in early[1:]:
            copy.wait()
    each(blocks, turn)

    pl.semaphore_wait(barrier, peers)

    exchange = pltpu.make_async_remote_copy(
        src_ref=turned.at[half],
        dst_ref=turned.at[half],
        send_sem=esem.at[0],
        recv_sem=esem.at[1],
        device_id=partner,
        device_id_type=MESH,
    )
    exchange.start()

    def transfer(source, target, send, receive, o):
        to = peer(o + 1)
        return pltpu.make_async_remote_copy(
            src_ref=source.at[to],
            dst_ref=target.at[me],
            send_sem=send,
            recv_sem=receive,
            device_id={"dev": to},
            device_id_type=MESH,
        )

    def rotations(o):
        return transfer(rot_ref, rrot, rot_sem.at[0], rot_sem.at[1], o)

    def messages(o):
        return transfer(msg, recv, msg_sem.at[0], msg_sem.at[1], o)

    def everything(source, target, sems):
        return pltpu.make_async_remote_copy(
            src_ref=source.at[pl.ds(0, peers - 1)],
            dst_ref=target.at[pl.ds(0, peers - 1)],
            send_sem=sems.at[0],
            recv_sem=sems.at[1],
            device_id={"dev": peer(1)},
            device_id_type=MESH,
        )

    all_rotations = everything(rot_ref, rrot, rot_sem)
    all_messages = everything(msg, recv, msg_sem)

    each_peer(peers, lambda o: rotations(o).start())
    rrot[me] = rot_ref[me]

    for copy in waits:
        copy.wait()
    for slot in range(ORDERS[0][1]):
        flipped = w0_raw[:, slot * LANES : (slot + 1) * LANES].T
        for side in (0, 1):
            w0[side, slot * HALF : (slot + 1) * HALF, :] = flipped[side * HALF : (side + 1) * HALF]
    for kind in (0, 1):
        for slot in range(ORDERS[3][1]):
            flipped = w2_raw[kind, :, slot * LANES : (slot + 1) * LANES].T
            for side in (0, 1):
                w2[
                    side,
                    slot * HALF : (slot + 1) * HALF,
                    kind * SPLIT : kind * SPLIT + flipped.shape[1],
                ] = flipped[side * HALF : (side + 1) * HALF]

    def product(side, block):
        def rows(order):
            start = STARTS[order]
            return turned[side, block, :, start : start + ORDERS[order][1] * HALF]

        def dot(lhs, rhs):
            return jnp.dot(lhs, rhs, preferred_element_type=jnp.float32)

        results = [dot(rows(0), w0[side])]
        for plus, ref, gap in ((1, w1, width), (3, w2, SPLIT)):
            pair = jnp.concatenate([rows(plus), rows(plus + 1)], axis=0)
            weights = ref[side]
            if weights.ndim == 3:
                weights = weights.reshape(-1, weights.shape[-1])
            both = dot(pair, weights)
            span = ORDERS[plus][1] * HALF
            results.append(both[:BLOCK, :span] - both[BLOCK:, gap : gap + span])
            results.append(both[:BLOCK, gap : gap + span] + both[BLOCK:, :span])
        return results

    def own(block):
        for order, value in enumerate(product(half, block)):
            start = STARTS[order]
            part_scr[block, :, start : start + value.shape[1]] = value

    def mix(block):
        for order, value in enumerate(product(1 - half, block)):
            start = STARTS[order]
            sent = SENT[order]
            y_scr[:, sent : sent + value.shape[1]] = (
                value + part_scr[block, :, start : start + value.shape[1]]
            )
        for index in range(group):
            msg[block * group + index] = y_scr[index * slots : (index + 1) * slots, :].astype(
                jnp.bfloat16
            )

    each(blocks, own)
    exchange.wait()
    each(blocks, mix)
    each_peer(peers, lambda o: messages(o).start())
    recv[me] = msg[me]

    all_rotations.wait_recv()

    def prepare(block):
        spread(rrot, block * group)

    def collect(block, add):
        for index in range(group):
            f_scr[index * slots : (index + 1) * slots, :] = recv[block * group + index].astype(
                jnp.float32
            )
        doubled = {}
        for slot in range(FRAME):
            tile, side = message_place(slot)
            value = f_scr[:, tile * LANES : (tile + 1) * LANES]
            turned = pltpu.roll(value, HALF, 1)
            doubled[slot] = (
                jnp.where(low_half, value, turned) if side == 0 else jnp.where(low_half, turned, value)
            )
        sums = [None] * TILES
        for slot, tile, number, which in PARTS:
            part = factor(number, which) * doubled[slot]
            sums[tile] = part if sums[tile] is None else sums[tile] + part
        for tile in range(TILES):
            back[:, tile * LANES : (tile + 1) * LANES] = sums[tile].astype(jnp.bfloat16)
        hot = (
            lax.broadcasted_iota(jnp.int32, (nodes, BLOCK), 0).astype(jnp.float32) == targets(block)
        ).astype(jnp.bfloat16)
        value = jnp.dot(hot, back[...], preferred_element_type=jnp.float32)
        total[...] = total[...] + value if add else value

    if blocks == 1:
        prepare(0)
        all_messages.wait_recv()
        collect(0, False)
    else:
        all_messages.wait_recv()
        total[...] = jnp.zeros_like(total)

        def one(block, carry):
            prepare(block)
            collect(block, True)
            return carry

        lax.fori_loop(0, blocks, one, 0)

    partial = None
    for tile in range(TILES):
        value = total[:, tile * LANES : (tile + 1) * LANES]
        partial = value * value if partial is None else partial + value * value
    sq[...] = partial
    share = pltpu.make_async_remote_copy(
        src_ref=sq,
        dst_ref=sq_other,
        send_sem=qsem.at[0],
        recv_sem=qsem.at[1],
        device_id=partner,
        device_id_type=MESH,
    )
    share.start()
    all_rotations.wait_send()
    all_messages.wait_send()
    share.wait()
    sums_ref[...] = sq[...] + sq_other[...]


def finish(chunks, x_ref, total, sums_ref, gain_ref, out_hbm, out_ref, sems):
    flat = x_ref.shape[1]
    mean_sq = jnp.sum(sums_ref[...], axis=1, keepdims=True) / (2 * flat)
    scale = lax.rsqrt(mean_sq + 1e-06)
    copies = []
    for index, (first, last) in enumerate(chunks):
        for start in range(first, last, LANES):
            cols = slice(start, min(start + LANES, last))
            normed = total[:, cols] * scale
            out_ref[:, cols] = (
                x_ref[:, cols].astype(jnp.float32) + gain_ref[:, cols] * normed
            ).astype(jnp.bfloat16)
        part = slice(first, last)
        copies.append(
            pltpu.make_async_copy(out_ref.at[:, part], out_hbm.at[:, part], sems.at[index])
        )
        copies[-1].start()
    for copy in copies:
        copy.wait()


def shards(node_features, src_node, dst_node, counts, rotation, w_zero, w_one, w_two, norm_gain):
    nodes, _, flat = node_features.shape
    peers, slots = src_node.shape[1:]
    edges = peers * slots
    blocks = edges // BLOCK
    x = node_features.reshape(nodes, flat)
    group = peers // blocks
    src = src_node.reshape(blocks, group, slots).swapaxes(1, 2)
    dst = dst_node.reshape(blocks, group, slots).swapaxes(1, 2)
    cnt = counts.reshape(blocks, 1, group)
    rot = rotation.reshape(peers, slots, ROT)
    w0 = w_zero.reshape(w_zero.shape[0], -1).T
    w1 = w_one.reshape(2, -1, 2, HALF, w_one.shape[-1])
    w2 = w_two.reshape(2, w_two.shape[1], -1).swapaxes(1, 2)
    vmem = pl.BlockSpec(memory_space=pltpu.VMEM)
    hbm = pl.BlockSpec(memory_space=pltpu.HBM)
    f32, bf16 = jnp.float32, jnp.bfloat16
    dma = pltpu.SemaphoreType.DMA
    operands = (x, rot, src, cnt, dst, w0, w1, w2)
    held, total, sums = pl.pallas_call(
        functools.partial(kernel, peers, slots),
        out_shape=(
            jax.ShapeDtypeStruct((nodes, flat), bf16),
            jax.ShapeDtypeStruct((nodes, WIDE), f32),
            jax.ShapeDtypeStruct((nodes, LANES), f32),
        ),
        in_specs=[hbm] * 8,
        out_specs=(vmem,) * 3,
        scratch_shapes=[
            pltpu.VMEM(rot.shape, bf16),
            pltpu.VMEM(src.shape, jnp.int32),
            pltpu.VMEM(cnt.shape, jnp.int32),
            pltpu.VMEM(dst.shape, jnp.int32),
            pltpu.VMEM(w0.shape, bf16),
            pltpu.VMEM(w2.shape, bf16),
            pltpu.VMEM((2, w0.shape[1] // 2, w0.shape[0]), bf16),
            pltpu.VMEM((2, w1.shape[1], HALF, 2 * w1.shape[-1]), bf16),
            pltpu.VMEM((2, w2.shape[2] // 2, 2 * SPLIT), bf16),
            pltpu.VMEM((2, LANES, 2 * LANES), bf16),
            pltpu.VMEM((BLOCK, 2 * LANES), f32),
            pltpu.VMEM((ALL_ROWS, LANES), bf16),
            pltpu.VMEM((ALL_ROWS, 2 * LANES), f32),
            pltpu.VMEM((BLOCK, WIDE), f32),
            pltpu.VMEM((2, blocks, BLOCK, len(PAIRS) * LANES), bf16),
            pltpu.VMEM((blocks, BLOCK, len(PAIRS) * LANES), f32),
            pltpu.VMEM((BLOCK, MESSAGE), f32),
            pltpu.VMEM((peers, slots, MESSAGE), bf16),
            pltpu.VMEM((peers, slots, MESSAGE), bf16),
            pltpu.VMEM((peers, slots, ROT), bf16),
            pltpu.VMEM((BLOCK, MESSAGE), f32),
            pltpu.VMEM((BLOCK, WIDE), bf16),
            pltpu.VMEM((nodes, LANES), f32),
            pltpu.VMEM((nodes, LANES), f32),
            dma((8,)),
            dma((2,)),
            dma((2,)),
            dma((2,)),
            dma((2,)),
        ],
        compiler_params=pltpu.CompilerParams(
            collective_id=0, has_side_effects=True, vmem_limit_bytes=VMEM_LIMIT
        ),
    )(*(pltpu.with_memory_space_constraint(operand, pltpu.HBM) for operand in operands))
    cut = (flat // LANES + 3) // 4 * LANES
    chunks = [(start, min(start + cut, flat)) for start in range(0, flat, cut)]
    out = pl.pallas_call(
        functools.partial(finish, chunks),
        out_shape=jax.ShapeDtypeStruct((nodes, flat), bf16),
        in_specs=[vmem] * 4,
        out_specs=hbm,
        scratch_shapes=[pltpu.VMEM((nodes, flat), bf16), dma((len(chunks),))],
        compiler_params=pltpu.CompilerParams(vmem_limit_bytes=VMEM_LIMIT),
    )(held, total, sums, norm_gain)
    return out.reshape(nodes, 1, flat)


def solution(mesh):
    return jax.shard_map(
        shards,
        mesh=mesh,
        in_specs=(
            P("dev", "rep", None),
            P("dev", None, None),
            P("dev", None, None),
            P("dev", None),
            P("dev", None, None, None),
            P(None, "rep", None),
            P(None, None, "rep", None),
            P(None, None, "rep", None),
            P("rep", None),
        ),
        out_specs=P("dev", "rep", None),
        check_vma=False,
    )
```

time: 17 us -> 15.9 us (0.935)
  local copies, waits for them, and re-layouts: 0.75 us -> 0.01 us
  Pallas kernels: 16.1 us -> 15.8 us
    unnamed x1 -> x2, local copies, waits for them, and re-layouts: 0.75 us -> 0.01 us
    pallas_call x1 -> x2, Pallas kernels: 16.1 us -> 15.8 us  [the longest x1 14.8 us: shards(): pl.pallas_call(functools.partial(kernel, peers, slots), out_shape=(jax.Sh...]
where the time goes in v2:
time: 15.9 us; the launch traced here: 15.8 us
  Pallas kernels  15.8 us (99%)
    pallas_call x1, Pallas kernels, shards(): pl.pallas_call(functools.partial(kernel, peers, slots), out_shape=(jax.Sh...  14.8 us
    pallas_call x1, Pallas kernels, shards(): pl.pallas_call(functools.partial(finish, chunks), out_shape=jax.ShapeDtyp...  0.9 us

profile of v2, /device:TPU:0, one launch (start us, length us, event | category | flops | bytes accessed | tf_op | source)
XLA Modules:
  0.0 15.8 jit_solution(6950342147854266963)
XLA Ops:
  0.0 0.0 copy-start
  0.0 14.8 %shard_map.91 = (bf16[64,3136]{1,0:T(8,128)(2,1)S(1)}, f32[64,3200]{1,0:T(8,128)S(1)}, f32[64,128]{1,0:T(8,128)S(1)}) custom-call(bf16[64,3136]{1,0:T(8,128)(2,1)} %bitcast.16, bf16[16,2,235]{2,1,0:T(2,128)(2,1)} %bitcast.17, s32[1,2,16]{2,1,0:T(2,128)} %bitcast.18, s32[1,1,16]{2,1,0:T(1,128)} %bitcast.20, s32[1,2,16]{2,1,0:T(2,128)} %bitcast.19, ...), custom_call_target="tpu_custom_call" | custom-call | tf_op jit(solution)/shard_map/pallas_call | solution.py:503
  14.9 0.0 copy-done
  14.9 0.9 %shard_map.92 = bf16[64,3136]{1,0:T(8,128)(2,1)} custom-call(bf16[64,3136]{1,0:T(8,128)(2,1)S(1)} %get-tuple-element.8.x_ref, f32[64,3200]{1,0:T(8,128)S(1)} %get-tuple-element.9.total, f32[64,128]{1,0:T(8,128)S(1)} %get-tuple-element.10.sums_ref, f32[1,3136]{1,0:T(1,128)S(1)} %copy-done), custom_call_target="tpu_custom_call" | custom-call | tf_op jit(solution)/shard_map/pallas_call | solution.py:549
Async XLA Ops:
  0.0 14.9 %copy-start = (f32[1,3136]{1,0:T(1,128)S(1)}, f32[1,3136]{1,0:T(1,128)}, u32[]{:S(2)}) copy-start(f32[1,3136]{1,0:T(1,128)} %gain_ref.1) | copy-start | bytes 37636

commit v3 on v2

--- a/solution.py
+++ b/solution.py
@@ -17,6 +17,7 @@
 MESSAGE = (FRAME + 1) // 2 * LANES
 VMEM_LIMIT = 40 * 1024 * 1024
 BLOCK = 32
+PIECE = 16
 MESH = pl.DeviceIdType.MESH
 ORDERS = ((0, 7), (7, 6), (13, 6), (19, 5), (24, 5))
 SEND_ORDER = (0, 4, 1, 2, 3)
@@ -64,7 +65,7 @@
 
 
 GROUPS, PARTS, SEGMENTS = listings()
-LOW_ROWS = BLOCK * sum(window == 0 for window, _, _ in GROUPS)
+LOW_GROUPS = sum(window == 0 for window, _, _ in GROUPS)
 ALL_ROWS = BLOCK * len(GROUPS)
 
 
@@ -100,18 +101,6 @@
     return place // 2, place % 2
 
 
-def far_first(count):
-    return sorted(range(1, count), key=lambda offset: -min(offset, count - offset))
-
-
-def each_peer(count, func):
-    if count <= 17:
-        for offset in far_first(count):
-            func(offset - 1)
-    else:
-        each(count - 1, func)
-
-
 def each(count, func):
     if count <= 16:
         for index in range(count):
@@ -128,6 +117,7 @@
     src_hbm,
     cnt_hbm,
     dst_hbm,
+    gain_hbm,
     w0_hbm,
     w1_hbm,
     w2_hbm,
@@ -138,6 +128,7 @@
     src_ref,
     cnt_ref,
     dst_ref,
+    gain_ref,
     w0_raw,
     w2_raw,
     w0,
@@ -172,8 +163,8 @@
     group = BLOCK // slots
     partner = {"rep": 1 - half}
 
-    def peer(offset):
-        return lax.rem(me + offset, peers)
+    def peer(index):
+        return index + lax.div(index + peers - me, peers)
 
     def load(index, src, dst):
         return pltpu.make_async_copy(src, dst, wsem.at[index])
@@ -184,13 +175,18 @@
         load(2, cnt_hbm, cnt_ref),
         load(3, x_hbm, x_ref),
     ]
-    late = [load(4, dst_hbm, dst_ref), load(5, w0_hbm, w0_raw), load(6, w2_hbm, w2_raw)]
+    late = [
+        load(4, dst_hbm, dst_ref),
+        load(5, w0_hbm, w0_raw),
+        load(6, w2_hbm, w2_raw),
+        load(8, gain_hbm, gain_ref),
+    ]
     width = w1_hbm.shape[-1]
     for side in (0, 1):
         for kind in (0, 1):
             cols = slice(kind * width, (kind + 1) * width)
             late.append(load(7, w1_hbm.at[kind, :, side], w1.at[side, :, :, cols]))
-    waits = late[:3] + [load(7, w1, w1)]
+    waits = late[:4] + [load(7, w1, w1)]
     for copy in early + late:
         copy.start()
     barrier = pltpu.get_barrier_semaphore()
@@ -198,12 +194,12 @@
     each(
         peers - 1,
         lambda o: pl.semaphore_signal(
-            barrier, inc=1, device_id={"dev": peer(o + 1)}, device_id_type=MESH
+            barrier, inc=1, device_id={"dev": peer(o)}, device_id_type=MESH
         ),
     )
 
-    lane = lax.broadcasted_iota(jnp.int32, (BLOCK, LANES), 1)
-    low_half = lane < HALF
+    def lanes(rows):
+        return lax.broadcasted_iota(jnp.int32, (rows, LANES), 1)
 
     y_scr[...] = jnp.zeros_like(y_scr)
     xg[:, flat:] = jnp.zeros((BLOCK, xg.shape[1] - flat), jnp.float32)
@@ -245,37 +241,38 @@
         spot = lax.broadcasted_iota(jnp.int32, (BLOCK, BLOCK), 1)
         return jnp.sum(jnp.where(row == spot, down, 0.0), axis=0, keepdims=True)
 
-    def spread(ref, start):
-        for index in range(group):
+    def spread(ref, start, edges):
+        for index in range(edges // slots):
             rot_scr[index * slots : (index + 1) * slots, 0:ROT] = ref[start + index].astype(
                 jnp.float32
             )
         for number, (window, first, last) in enumerate(GROUPS):
-            spots = lane + window * LANES
-            rows = rot_scr[:, window * LANES : (window + 1) * LANES]
-            entries[number * BLOCK : (number + 1) * BLOCK, :] = jnp.where(
+            spots = lanes(edges) + window * LANES
+            rows = rot_scr[0:edges, window * LANES : (window + 1) * LANES]
+            entries[number * edges : (number + 1) * edges, :] = jnp.where(
                 (spots >= first) & (spots <= last), rows, 0.0
             ).astype(jnp.bfloat16)
-        for window, rows in enumerate((slice(0, LOW_ROWS), slice(LOW_ROWS, ALL_ROWS))):
+        cut = LOW_GROUPS * edges
+        for window, rows in enumerate((slice(0, cut), slice(cut, len(GROUPS) * edges))):
             mult[rows] = jnp.dot(
                 entries[rows], expand[window], preferred_element_type=jnp.float32
             )
 
-    def factor(number, which):
-        return mult[number * BLOCK : (number + 1) * BLOCK, which * LANES : (which + 1) * LANES]
+    def factor(number, which, edges):
+        return mult[number * edges : (number + 1) * edges, which * LANES : (which + 1) * LANES]
 
     def turn(block):
-        spread(rot_ref, block * group)
-        if block is first_block:
-            for copy in early[1:]:
-                copy.wait()
+        low_half = lanes(BLOCK) < HALF
         hot = (
             lax.broadcasted_iota(jnp.int32, (BLOCK, nodes), 1).astype(jnp.float32) == sources(block)
         ).astype(jnp.bfloat16)
+        spread(rot_ref, block * group, BLOCK)
+        if block is first_block:
+            early[3].wait()
         xg[:, 0:flat] = jnp.dot(hot, x_ref[...], preferred_element_type=jnp.float32)
         sums = [None] * FRAME
         for slot, tile, number, which in PARTS:
-            part = factor(number, which) * xg[:, tile * LANES : (tile + 1) * LANES]
+            part = factor(number, which, BLOCK) * xg[:, tile * LANES : (tile + 1) * LANES]
             sums[slot] = part if sums[slot] is None else sums[slot] + part
         for pair, (one, two) in enumerate(PAIRS):
             kept = jnp.where(low_half, sums[one], sums[two])
@@ -284,11 +281,11 @@
                 kept + pltpu.roll(moved, HALF, 1)
             ).astype(jnp.bfloat16)
 
-    early[0].wait()
+    for copy in early[:3]:
+        copy.wait()
     first_block = 0 if blocks <= 16 else None
     if first_block is None:
-        for copy in early[1:]:
-            copy.wait()
+        early[3].wait()
     each(blocks, turn)
 
     pl.semaphore_wait(barrier, peers)
@@ -303,38 +300,32 @@
     )
     exchange.start()
 
-    def transfer(source, target, send, receive, o):
-        to = peer(o + 1)
+    share_of = lax.div(me, peers // 2)
+
+    def transfer(source, target, sems, o):
+        to = peer(o)
         return pltpu.make_async_remote_copy(
             src_ref=source.at[to],
             dst_ref=target.at[me],
-            send_sem=send,
-            recv_sem=receive,
+            send_sem=sems.at[2],
+            recv_sem=sems.at[share_of],
             device_id={"dev": to},
             device_id_type=MESH,
         )
 
-    def rotations(o):
-        return transfer(rot_ref, rrot, rot_sem.at[0], rot_sem.at[1], o)
-
-    def messages(o):
-        return transfer(msg, recv, msg_sem.at[0], msg_sem.at[1], o)
-
-    def everything(source, target, sems):
-        return pltpu.make_async_remote_copy(
-            src_ref=source.at[pl.ds(0, peers - 1)],
-            dst_ref=target.at[pl.ds(0, peers - 1)],
-            send_sem=sems.at[0],
-            recv_sem=sems.at[1],
-            device_id={"dev": peer(1)},
-            device_id_type=MESH,
-        )
-
-    all_rotations = everything(rot_ref, rrot, rot_sem)
-    all_messages = everything(msg, recv, msg_sem)
-
-    each_peer(peers, lambda o: rotations(o).start())
-    rrot[me] = rot_ref[me]
+    def keep(source, target, sems):
+        return pltpu.make_async_copy(source.at[me], target.at[me], sems.at[share_of])
+
+    def arrived(target, sems, part):
+        span = target.at[pl.ds(part * (peers // 2), peers // 2)]
+        return pltpu.make_async_copy(span, span, sems.at[part])
+
+    def sent(source, sems):
+        span = source.at[pl.ds(0, peers - 1)]
+        return pltpu.make_async_copy(span, span, sems.at[2])
+
+    each(peers - 1, lambda o: transfer(rot_ref, rrot, rot_sem, o).start())
+    keep(rot_ref, rrot, rot_sem).start()
 
     for copy in waits:
         copy.wait()
@@ -392,19 +383,13 @@
     each(blocks, own)
     exchange.wait()
     each(blocks, mix)
-    each_peer(peers, lambda o: messages(o).start())
-    recv[me] = msg[me]
-
-    all_rotations.wait_recv()
-
-    def prepare(block):
-        spread(rrot, block * group)
-
-    def collect(block, add):
-        for index in range(group):
-            f_scr[index * slots : (index + 1) * slots, :] = recv[block * group + index].astype(
-                jnp.float32
-            )
+    each(peers - 1, lambda o: transfer(msg, recv, msg_sem, o).start())
+    keep(msg, recv, msg_sem).start()
+
+    def collect(start):
+        low_half = lanes(PIECE) < HALF
+        for index in range(PIECE // slots):
+            f_scr[index * slots : (index + 1) * slots, :] = recv[start + index].astype(jnp.float32)
         doubled = {}
         for slot in range(FRAME):
             tile, side = message_place(slot)
@@ -415,35 +400,51 @@
             )
         sums = [None] * TILES
         for slot, tile, number, which in PARTS:
-            part = factor(number, which) * doubled[slot]
+            part = factor(number, which, PIECE) * doubled[slot]
             sums[tile] = part if sums[tile] is None else sums[tile] + part
+        first = pl.multiple_of(start * slots, PIECE)
         for tile in range(TILES):
-            back[:, tile * LANES : (tile + 1) * LANES] = sums[tile].astype(jnp.bfloat16)
-        hot = (
-            lax.broadcasted_iota(jnp.int32, (nodes, BLOCK), 0).astype(jnp.float32) == targets(block)
-        ).astype(jnp.bfloat16)
-        value = jnp.dot(hot, back[...], preferred_element_type=jnp.float32)
-        total[...] = total[...] + value if add else value
-
-    if blocks == 1:
-        prepare(0)
-        all_messages.wait_recv()
-        collect(0, False)
-    else:
-        all_messages.wait_recv()
-        total[...] = jnp.zeros_like(total)
-
-        def one(block, carry):
-            prepare(block)
-            collect(block, True)
-            return carry
-
-        lax.fori_loop(0, blocks, one, 0)
-
+            back[pl.ds(first, PIECE), tile * LANES : (tile + 1) * LANES] = sums[tile].astype(
+                jnp.bfloat16
+            )
+
+    wide = PIECE // slots
+    pieces = peers // 2 // wide
+    for part in (0, 1):
+        arrived(rrot, rot_sem, part).wait()
+        base = part * (peers // 2)
+        if pieces == 1:
+            spread(rrot, base, PIECE)
+            arrived(recv, msg_sem, part).wait()
+            collect(base)
+        else:
+            arrived(recv, msg_sem, part).wait()
+
+            def one(piece, carry):
+                spread(rrot, base + piece * wide, PIECE)
+                collect(base + piece * wide)
+                return carry
+
+            lax.fori_loop(0, pieces, one, 0)
+
+    hot = jnp.concatenate(
+        [
+            (
+                lax.broadcasted_iota(jnp.int32, (nodes, BLOCK), 0).astype(jnp.float32)
+                == targets(block)
+            ).astype(jnp.bfloat16)
+            for block in range(blocks)
+        ],
+        axis=1,
+    )
     partial = None
-    for tile in range(TILES):
-        value = total[:, tile * LANES : (tile + 1) * LANES]
-        partial = value * value if partial is None else partial + value * value
+    for start in range(0, WIDE, 2 * LANES):
+        cols = slice(start, min(start + 2 * LANES, WIDE))
+        value = jnp.dot(hot, back[:, cols], preferred_element_type=jnp.float32)
+        total[:, cols] = value
+        for part in range(0, cols.stop - start, LANES):
+            square = value[:, part : part + LANES] * value[:, part : part + LANES]
+            partial = square if partial is None else partial + square
     sq[...] = partial
     share = pltpu.make_async_remote_copy(
         src_ref=sq,
@@ -454,13 +455,16 @@
         device_id_type=MESH,
     )
     share.start()
-    all_rotations.wait_send()
-    all_messages.wait_send()
+    for start in range(0, flat, LANES):
+        cols = slice(start, min(start + LANES, flat))
+        total[:, cols] = total[:, cols] * gain_ref[:, cols]
+    sent(rot_ref, rot_sem).wait()
+    sent(msg, msg_sem).wait()
     share.wait()
     sums_ref[...] = sq[...] + sq_other[...]
 
 
-def finish(chunks, x_ref, total, sums_ref, gain_ref, out_hbm, out_ref, sems):
+def finish(chunks, x_ref, total, sums_ref, out_hbm, out_ref, sems):
     flat = x_ref.shape[1]
     mean_sq = jnp.sum(sums_ref[...], axis=1, keepdims=True) / (2 * flat)
     scale = lax.rsqrt(mean_sq + 1e-06)
@@ -469,9 +473,7 @@
         for start in range(first, last, LANES):
             cols = slice(start, min(start + LANES, last))
             normed = total[:, cols] * scale
-            out_ref[:, cols] = (
-                x_ref[:, cols].astype(jnp.float32) + gain_ref[:, cols] * normed
-            ).astype(jnp.bfloat16)
+            out_ref[:, cols] = (x_ref[:, cols].astype(jnp.float32) + normed).astype(jnp.bfloat16)
         part = slice(first, last)
         copies.append(
             pltpu.make_async_copy(out_ref.at[:, part], out_hbm.at[:, part], sems.at[index])
@@ -499,7 +501,7 @@
     hbm = pl.BlockSpec(memory_space=pltpu.HBM)
     f32, bf16 = jnp.float32, jnp.bfloat16
     dma = pltpu.SemaphoreType.DMA
-    operands = (x, rot, src, cnt, dst, w0, w1, w2)
+    operands = (x, rot, src, cnt, dst, norm_gain, w0, w1, w2)
     held, total, sums = pl.pallas_call(
         functools.partial(kernel, peers, slots),
         out_shape=(
@@ -507,13 +509,14 @@
             jax.ShapeDtypeStruct((nodes, WIDE), f32),
             jax.ShapeDtypeStruct((nodes, LANES), f32),
         ),
-        in_specs=[hbm] * 8,
+        in_specs=[hbm] * 9,
         out_specs=(vmem,) * 3,
         scratch_shapes=[
             pltpu.VMEM(rot.shape, bf16),
             pltpu.VMEM(src.shape, jnp.int32),
             pltpu.VMEM(cnt.shape, jnp.int32),
             pltpu.VMEM(dst.shape, jnp.int32),
+            pltpu.VMEM(norm_gain.shape, f32),
             pltpu.VMEM(w0.shape, bf16),
             pltpu.VMEM(w2.shape, bf16),
             pltpu.VMEM((2, w0.shape[1] // 2, w0.shape[0]), bf16),
@@ -530,14 +533,14 @@
             pltpu.VMEM((peers, slots, MESSAGE), bf16),
             pltpu.VMEM((peers, slots, MESSAGE), bf16),
             pltpu.VMEM((peers, slots, ROT), bf16),
-            pltpu.VMEM((BLOCK, MESSAGE), f32),
-            pltpu.VMEM((BLOCK, WIDE), bf16),
+            pltpu.VMEM((PIECE, MESSAGE), f32),
+            pltpu.VMEM((edges, WIDE), bf16),
             pltpu.VMEM((nodes, LANES), f32),
             pltpu.VMEM((nodes, LANES), f32),
-            dma((8,)),
+            dma((9,)),
             dma((2,)),
-            dma((2,)),
-            dma((2,)),
+            dma((3,)),
+            dma((3,)),
             dma((2,)),
         ],
         compiler_params=pltpu.CompilerParams(
@@ -549,11 +552,11 @@
     out = pl.pallas_call(
         functools.partial(finish, chunks),
         out_shape=jax.ShapeDtypeStruct((nodes, flat), bf16),
-        in_specs=[vmem] * 4,
+        in_specs=[vmem] * 3,
         out_specs=hbm,
         scratch_shapes=[pltpu.VMEM((nodes, flat), bf16), dma((len(chunks),))],
         compiler_params=pltpu.CompilerParams(vmem_limit_bytes=VMEM_LIMIT),
-    )(held, total, sums, norm_gain)
+    )(held, total, sums)
     return out.reshape(nodes, 1, flat)
 
 

time: 15.9 us -> 14.6 us (0.918)
  Pallas kernels: 15.8 us -> 14.3 us
    pallas_call x1, Pallas kernels: 14.8 us -> 13.4 us  [shards(): pl.pallas_call(functools.partial(kernel, peers, slots), out_shape=(jax.Sh...]
where the time goes in v3:
time: 14.6 us; the launch traced here: 14.3 us
  Pallas kernels  14.3 us (98%)
    pallas_call x1, Pallas kernels, shards(): pl.pallas_call(functools.partial(kernel, peers, slots), out_shape=(jax.Sh...  13.4 us
    pallas_call x1, Pallas kernels, shards(): pl.pallas_call(functools.partial(finish, chunks), out_shape=jax.ShapeDtyp...  0.89 us

profile of v3, /device:TPU:0, one launch (start us, length us, event | category | flops | bytes accessed | tf_op | source)
XLA Modules:
  0.0 14.3 jit_solution(8322689637347394291)
XLA Ops:
  0.0 13.4 %shard_map.91 = (bf16[64,3136]{1,0:T(8,128)(2,1)S(1)}, f32[64,3200]{1,0:T(8,128)S(1)}, f32[64,128]{1,0:T(8,128)S(1)}) custom-call(bf16[64,3136]{1,0:T(8,128)(2,1)} %bitcast.16, bf16[16,2,235]{2,1,0:T(2,128)(2,1)} %bitcast.17, s32[1,2,16]{2,1,0:T(2,128)} %bitcast.18, s32[1,1,16]{2,1,0:T(1,128)} %bitcast.20, s32[1,2,16]{2,1,0:T(2,128)} %bitcast.19, ...), custom_call_target="tpu_custom_call" | custom-call | tf_op jit(solution)/shard_map/pallas_call | solution.py:505
  13.4 0.9 %shard_map.92 = bf16[64,3136]{1,0:T(8,128)(2,1)} custom-call(bf16[64,3136]{1,0:T(8,128)(2,1)S(1)} %get-tuple-element.8.x_ref, f32[64,3200]{1,0:T(8,128)S(1)} %get-tuple-element.9.total, f32[64,128]{1,0:T(8,128)S(1)} %get-tuple-element.10.sums_ref), custom_call_target="tpu_custom_call" | custom-call | tf_op jit(solution)/shard_map/pallas_call | solution.py:552

commit v4 on v3

--- a/solution.py
+++ b/solution.py
@@ -37,6 +37,7 @@
 
 def listings():
     groups = []
+    alone = []
     parts = []
     segments = []
     spot = 0
@@ -51,6 +52,10 @@
             for quad in range(first // 4, (first + span - 1) // 4 + 1):
                 low = base + max(4 * quad, first)
                 high = base + min(4 * quad + 3, first + span - 1)
+                if low == high and (low - base) % 2 == 0:
+                    parts.append((slot, 2 * quad, len(alone), None))
+                    alone.append(low)
+                    continue
                 for window in (0, 1):
                     start = max(low, window * LANES)
                     end = min(high, window * LANES + LANES - 1)
@@ -61,10 +66,10 @@
                                 parts.append((slot, tile, len(groups), which))
                         groups.append((window, start, end))
         spot += span * (2 * reach + 1)
-    return groups, parts, segments
-
-
-GROUPS, PARTS, SEGMENTS = listings()
+    return groups, alone, parts, segments
+
+
+GROUPS, ALONE, PARTS, SEGMENTS = listings()
 LOW_GROUPS = sum(window == 0 for window, _, _ in GROUPS)
 ALL_ROWS = BLOCK * len(GROUPS)
 
@@ -138,6 +143,7 @@
     rot_scr,
     entries,
     mult,
+    single,
     xg,
     turned,
     part_scr,
@@ -163,7 +169,12 @@
     group = BLOCK // slots
     partner = {"rep": 1 - half}
 
+    side = lax.div(me, peers // 2)
+
     def peer(index):
+        step, odd = index // 2, index % 2
+        mixed = (1 - odd) * step + odd * (peers - 2 - step)
+        index = side * index + (1 - side) * mixed
         return index + lax.div(index + peers - me, peers)
 
     def load(index, src, dst):
@@ -175,19 +186,19 @@
         load(2, cnt_hbm, cnt_ref),
         load(3, x_hbm, x_ref),
     ]
-    late = [
-        load(4, dst_hbm, dst_ref),
+    late = []
+    width = w1_hbm.shape[-1]
+    for part in (0, 1):
+        for kind in (0, 1):
+            cols = slice(kind * width, (kind + 1) * width)
+            late.append(load(7, w1_hbm.at[kind, :, part], w1.at[part, :, :, cols]))
+    late += [
         load(5, w0_hbm, w0_raw),
         load(6, w2_hbm, w2_raw),
+        load(4, dst_hbm, dst_ref),
         load(8, gain_hbm, gain_ref),
     ]
-    width = w1_hbm.shape[-1]
-    for side in (0, 1):
-        for kind in (0, 1):
-            cols = slice(kind * width, (kind + 1) * width)
-            late.append(load(7, w1_hbm.at[kind, :, side], w1.at[side, :, :, cols]))
-    waits = late[:4] + [load(7, w1, w1)]
-    for copy in early + late:
+    for copy in (early[3], *early[:3]):
         copy.start()
     barrier = pltpu.get_barrier_semaphore()
     pl.semaphore_signal(barrier, inc=1, device_id=partner, device_id_type=MESH)
@@ -210,11 +221,14 @@
         for start, offset in SEGMENTS:
             shift = jnp.where(entry >= start, offset, shift)
         place = lax.rem(entry + shift, 4)
-        for side in (0, 1):
-            hit = place == lax.div(spot, HALF) + 2 * side
-            expand[window, :, side * LANES : (side + 1) * LANES] = jnp.where(
+        for part in (0, 1):
+            hit = place == lax.div(spot, HALF) + 2 * part
+            expand[window, :, part * LANES : (part + 1) * LANES] = jnp.where(
                 hit, 1.0, 0.0
             ).astype(jnp.bfloat16)
+
+    for copy in late:
+        copy.start()
 
     def column(rows):
         row = lax.broadcasted_iota(jnp.int32, (BLOCK, group), 0)
@@ -241,34 +255,52 @@
         spot = lax.broadcasted_iota(jnp.int32, (BLOCK, BLOCK), 1)
         return jnp.sum(jnp.where(row == spot, down, 0.0), axis=0, keepdims=True)
 
-    def spread(ref, start, edges):
+    def place(ref, start, edges, spot=0):
+        base = spot * edges
         for index in range(edges // slots):
-            rot_scr[index * slots : (index + 1) * slots, 0:ROT] = ref[start + index].astype(
-                jnp.float32
-            )
+            first = base + index * slots
+            rot_scr[first : first + slots, 0:ROT] = ref[start + index].astype(jnp.float32)
         for number, (window, first, last) in enumerate(GROUPS):
             spots = lanes(edges) + window * LANES
-            rows = rot_scr[0:edges, window * LANES : (window + 1) * LANES]
-            entries[number * edges : (number + 1) * edges, :] = jnp.where(
+            rows = rot_scr[base : base + edges, window * LANES : (window + 1) * LANES]
+            first_row = (spot * len(GROUPS) + number) * edges
+            entries[first_row : first_row + edges, :] = jnp.where(
                 (spots >= first) & (spots <= last), rows, 0.0
             ).astype(jnp.bfloat16)
-        cut = LOW_GROUPS * edges
-        for window, rows in enumerate((slice(0, cut), slice(cut, len(GROUPS) * edges))):
-            mult[rows] = jnp.dot(
-                entries[rows], expand[window], preferred_element_type=jnp.float32
+
+    def spread(edges, spot=0):
+        base = spot * edges
+        low = base * len(GROUPS)
+        cut = low + LOW_GROUPS * edges
+        high = low + len(GROUPS) * edges
+        for window, span in enumerate((slice(low, cut), slice(cut, high))):
+            mult[span] = jnp.dot(
+                entries[span], expand[window], preferred_element_type=jnp.float32
             )
-
-    def factor(number, which, edges):
-        return mult[number * edges : (number + 1) * edges, which * LANES : (which + 1) * LANES]
+        for number, entry in enumerate(ALONE):
+            value = rot_scr[base : base + edges, entry : entry + 1]
+            value = jnp.broadcast_to(value, (edges, LANES))
+            first_row = (spot * len(ALONE) + number) * edges
+            single[first_row : first_row + edges, :] = jnp.where(
+                lanes(edges) < HALF, value, 0.0
+            )
+
+    def factor(number, which, edges, spot=0):
+        number += spot * len(ALONE if which is None else GROUPS)
+        span = slice(number * edges, (number + 1) * edges)
+        if which is None:
+            return single[span, :]
+        return mult[span, which * LANES : (which + 1) * LANES]
 
     def turn(block):
         low_half = lanes(BLOCK) < HALF
         hot = (
             lax.broadcasted_iota(jnp.int32, (BLOCK, nodes), 1).astype(jnp.float32) == sources(block)
         ).astype(jnp.bfloat16)
-        spread(rot_ref, block * group, BLOCK)
+        place(rot_ref, block * group, BLOCK)
         if block is first_block:
             early[3].wait()
+        spread(BLOCK)
         xg[:, 0:flat] = jnp.dot(hot, x_ref[...], preferred_element_type=jnp.float32)
         sums = [None] * FRAME
         for slot, tile, number, which in PARTS:
@@ -300,21 +332,19 @@
     )
     exchange.start()
 
-    share_of = lax.div(me, peers // 2)
-
     def transfer(source, target, sems, o):
         to = peer(o)
         return pltpu.make_async_remote_copy(
             src_ref=source.at[to],
             dst_ref=target.at[me],
             send_sem=sems.at[2],
-            recv_sem=sems.at[share_of],
+            recv_sem=sems.at[side],
             device_id={"dev": to},
             device_id_type=MESH,
         )
 
     def keep(source, target, sems):
-        return pltpu.make_async_copy(source.at[me], target.at[me], sems.at[share_of])
+        return pltpu.make_async_copy(source.at[me], target.at[me], sems.at[side])
 
     def arrived(target, sems, part):
         span = target.at[pl.ds(part * (peers // 2), peers // 2)]
@@ -327,66 +357,73 @@
     each(peers - 1, lambda o: transfer(rot_ref, rrot, rot_sem, o).start())
     keep(rot_ref, rrot, rot_sem).start()
 
-    for copy in waits:
-        copy.wait()
+    def rows(part, block, order):
+        start = STARTS[order]
+        return turned[part, block, :, start : start + ORDERS[order][1] * HALF]
+
+    def product(part, block, order):
+        if order == 0:
+            lhs = rows(part, block, order)
+            return [(0, jnp.dot(lhs, w0[part], preferred_element_type=jnp.float32))]
+        lhs = jnp.concatenate(
+            [rows(part, block, order), rows(part, block, order + 1)], axis=0
+        )
+        rhs, gap = (w1[part], width) if order == 1 else (w2[part], SPLIT)
+        if rhs.ndim == 3:
+            rhs = rhs.reshape(-1, rhs.shape[-1])
+        both = jnp.dot(lhs, rhs, preferred_element_type=jnp.float32)
+        span = ORDERS[order][1] * HALF
+        plus = both[:BLOCK, :span] - both[BLOCK:, gap : gap + span]
+        minus = both[:BLOCK, gap : gap + span] + both[BLOCK:, :span]
+        return [(order, plus), (order + 1, minus)]
+
+    def own(order):
+        def one(block):
+            for spot, value in product(half, block, order):
+                start = STARTS[spot]
+                part_scr[block, :, start : start + value.shape[1]] = value
+
+        return one
+
+    load(7, w1, w1).wait()
+    late[4].wait()
     for slot in range(ORDERS[0][1]):
         flipped = w0_raw[:, slot * LANES : (slot + 1) * LANES].T
-        for side in (0, 1):
-            w0[side, slot * HALF : (slot + 1) * HALF, :] = flipped[side * HALF : (side + 1) * HALF]
+        for part in (0, 1):
+            w0[part, slot * HALF : (slot + 1) * HALF, :] = flipped[part * HALF : (part + 1) * HALF]
+    each(blocks, own(1))
+    late[5].wait()
     for kind in (0, 1):
         for slot in range(ORDERS[3][1]):
             flipped = w2_raw[kind, :, slot * LANES : (slot + 1) * LANES].T
-            for side in (0, 1):
+            for part in (0, 1):
                 w2[
-                    side,
+                    part,
                     slot * HALF : (slot + 1) * HALF,
                     kind * SPLIT : kind * SPLIT + flipped.shape[1],
-                ] = flipped[side * HALF : (side + 1) * HALF]
-
-    def product(side, block):
-        def rows(order):
-            start = STARTS[order]
-            return turned[side, block, :, start : start + ORDERS[order][1] * HALF]
-
-        def dot(lhs, rhs):
-            return jnp.dot(lhs, rhs, preferred_element_type=jnp.float32)
-
-        results = [dot(rows(0), w0[side])]
-        for plus, ref, gap in ((1, w1, width), (3, w2, SPLIT)):
-            pair = jnp.concatenate([rows(plus), rows(plus + 1)], axis=0)
-            weights = ref[side]
-            if weights.ndim == 3:
-                weights = weights.reshape(-1, weights.shape[-1])
-            both = dot(pair, weights)
-            span = ORDERS[plus][1] * HALF
-            results.append(both[:BLOCK, :span] - both[BLOCK:, gap : gap + span])
-            results.append(both[:BLOCK, gap : gap + span] + both[BLOCK:, :span])
-        return results
-
-    def own(block):
-        for order, value in enumerate(product(half, block)):
-            start = STARTS[order]
-            part_scr[block, :, start : start + value.shape[1]] = value
+                ] = flipped[part * HALF : (part + 1) * HALF]
+    each(blocks, own(0))
+    each(blocks, own(3))
 
     def mix(block):
-        for order, value in enumerate(product(1 - half, block)):
-            start = STARTS[order]
-            sent = SENT[order]
-            y_scr[:, sent : sent + value.shape[1]] = (
-                value + part_scr[block, :, start : start + value.shape[1]]
-            )
+        for order in (0, 1, 3):
+            for spot, value in product(1 - half, block, order):
+                start = STARTS[spot]
+                sent = SENT[spot]
+                y_scr[:, sent : sent + value.shape[1]] = (
+                    value + part_scr[block, :, start : start + value.shape[1]]
+                )
         for index in range(group):
             msg[block * group + index] = y_scr[index * slots : (index + 1) * slots, :].astype(
                 jnp.bfloat16
             )
 
-    each(blocks, own)
     exchange.wait()
     each(blocks, mix)
     each(peers - 1, lambda o: transfer(msg, recv, msg_sem, o).start())
     keep(msg, recv, msg_sem).start()
 
-    def collect(start):
+    def collect(start, spot=0):
         low_half = lanes(PIECE) < HALF
         for index in range(PIECE // slots):
             f_scr[index * slots : (index + 1) * slots, :] = recv[start + index].astype(jnp.float32)
@@ -400,7 +437,7 @@
             )
         sums = [None] * TILES
         for slot, tile, number, which in PARTS:
-            part = factor(number, which, PIECE) * doubled[slot]
+            part = factor(number, which, PIECE, spot) * doubled[slot]
             sums[tile] = part if sums[tile] is None else sums[tile] + part
         first = pl.multiple_of(start * slots, PIECE)
         for tile in range(TILES):
@@ -410,18 +447,25 @@
 
     wide = PIECE // slots
     pieces = peers // 2 // wide
-    for part in (0, 1):
-        arrived(rrot, rot_sem, part).wait()
-        base = part * (peers // 2)
-        if pieces == 1:
-            spread(rrot, base, PIECE)
+    late[6].wait()
+    late[7].wait()
+    if pieces == 1:
+        for part in (0, 1):
+            arrived(rrot, rot_sem, part).wait()
+            place(rrot, part * wide, PIECE, part)
+            spread(PIECE, part)
+        for part in (0, 1):
             arrived(recv, msg_sem, part).wait()
-            collect(base)
-        else:
+            collect(part * wide, part)
+    else:
+        for part in (0, 1):
+            arrived(rrot, rot_sem, part).wait()
             arrived(recv, msg_sem, part).wait()
+            base = part * (peers // 2)
 
             def one(piece, carry):
-                spread(rrot, base + piece * wide, PIECE)
+                place(rrot, base + piece * wide, PIECE)
+                spread(PIECE)
                 collect(base + piece * wide)
                 return carry
 
@@ -526,6 +570,7 @@
             pltpu.VMEM((BLOCK, 2 * LANES), f32),
             pltpu.VMEM((ALL_ROWS, LANES), bf16),
             pltpu.VMEM((ALL_ROWS, 2 * LANES), f32),
+            pltpu.VMEM((BLOCK * len(ALONE), LANES), f32),
             pltpu.VMEM((BLOCK, WIDE), f32),
             pltpu.VMEM((2, blocks, BLOCK, len(PAIRS) * LANES), bf16),
             pltpu.VMEM((blocks, BLOCK, len(PAIRS) * LANES), f32),

time: 14.6 us -> 14.4 us (0.986)
  no operation moved by 1% of the time
where the time goes in v4:
time: 14.4 us; the launch traced here: 14.2 us
  Pallas kernels  14.2 us (99%)
    pallas_call x1, Pallas kernels, shards(): pl.pallas_call(functools.partial(kernel, peers, slots), out_shape=(jax.Sh...  13.3 us
    pallas_call x1, Pallas kernels, shards(): pl.pallas_call(functools.partial(finish, chunks), out_shape=jax.ShapeDtyp...  0.89 us

profile of v4, /device:TPU:0, one launch (start us, length us, event | category | flops | bytes accessed | tf_op | source)
XLA Modules:
  0.0 14.2 jit_solution(6472693697481013972)
XLA Ops:
  0.0 13.3 %shard_map.91 = (bf16[64,3136]{1,0:T(8,128)(2,1)S(1)}, f32[64,3200]{1,0:T(8,128)S(1)}, f32[64,128]{1,0:T(8,128)S(1)}) custom-call(bf16[64,3136]{1,0:T(8,128)(2,1)} %bitcast.16, bf16[16,2,235]{2,1,0:T(2,128)(2,1)} %bitcast.17, s32[1,2,16]{2,1,0:T(2,128)} %bitcast.18, s32[1,1,16]{2,1,0:T(1,128)} %bitcast.20, s32[1,2,16]{2,1,0:T(2,128)} %bitcast.19, ...), custom_call_target="tpu_custom_call" | custom-call | tf_op jit(solution)/shard_map/pallas_call | solution.py:549
  13.3 0.9 %shard_map.92 = bf16[64,3136]{1,0:T(8,128)(2,1)} custom-call(bf16[64,3136]{1,0:T(8,128)(2,1)S(1)} %get-tuple-element.8.x_ref, f32[64,3200]{1,0:T(8,128)S(1)} %get-tuple-element.9.total, f32[64,128]{1,0:T(8,128)S(1)} %get-tuple-element.10.sums_ref), custom_call_target="tpu_custom_call" | custom-call | tf_op jit(solution)/shard_map/pallas_call | solution.py:597

commit v5 on v4

--- a/solution.py
+++ b/solution.py
@@ -172,6 +172,7 @@
     side = lax.div(me, peers // 2)
 
     def peer(index):
+        index = lax.rem(index + half * (peers - 1 - peers // 2), peers - 1)
         step, odd = index // 2, index % 2
         mixed = (1 - odd) * step + odd * (peers - 2 - step)
         index = side * index + (1 - side) * mixed
@@ -406,19 +407,21 @@
     each(blocks, own(3))
 
     def mix(block):
-        for order in (0, 1, 3):
-            for spot, value in product(1 - half, block, order):
-                start = STARTS[spot]
-                sent = SENT[spot]
-                y_scr[:, sent : sent + value.shape[1]] = (
-                    value + part_scr[block, :, start : start + value.shape[1]]
-                )
+        values = []
+        for order in (3, 1, 0):
+            values += product(1 - half, block, order)
+        for spot, value in values:
+            start = STARTS[spot]
+            sent = SENT[spot]
+            y_scr[:, sent : sent + value.shape[1]] = (
+                value + part_scr[block, :, start : start + value.shape[1]]
+            )
         for index in range(group):
             msg[block * group + index] = y_scr[index * slots : (index + 1) * slots, :].astype(
                 jnp.bfloat16
             )
 
-    exchange.wait()
+    exchange.wait_recv()
     each(blocks, mix)
     each(peers - 1, lambda o: transfer(msg, recv, msg_sem, o).start())
     keep(msg, recv, msg_sem).start()
@@ -502,6 +505,7 @@
     for start in range(0, flat, LANES):
         cols = slice(start, min(start + LANES, flat))
         total[:, cols] = total[:, cols] * gain_ref[:, cols]
+    exchange.wait_send()
     sent(rot_ref, rot_sem).wait()
     sent(msg, msg_sem).wait()
     share.wait()

time: 14.4 us -> 14.3 us (level)
  no operation moved by 1% of the time
where the time goes in v5:
time: 14.3 us; the launch traced here: 14.1 us
  Pallas kernels  14.1 us (99%)
    pallas_call x1, Pallas kernels, shards(): pl.pallas_call(functools.partial(kernel, peers, slots), out_shape=(jax.Sh...  13.2 us
    pallas_call x1, Pallas kernels, shards(): pl.pallas_call(functools.partial(finish, chunks), out_shape=jax.ShapeDtyp...  0.89 us

profile of v5, /device:TPU:0, one launch (start us, length us, event | category | flops | bytes accessed | tf_op | source)
XLA Modules:
  0.0 14.1 jit_solution(794686442075107763)
XLA Ops:
  0.0 13.2 %shard_map.91 = (bf16[64,3136]{1,0:T(8,128)(2,1)S(1)}, f32[64,3200]{1,0:T(8,128)S(1)}, f32[64,128]{1,0:T(8,128)S(1)}) custom-call(bf16[64,3136]{1,0:T(8,128)(2,1)} %bitcast.16, bf16[16,2,235]{2,1,0:T(2,128)(2,1)} %bitcast.17, s32[1,2,16]{2,1,0:T(2,128)} %bitcast.18, s32[1,1,16]{2,1,0:T(1,128)} %bitcast.20, s32[1,2,16]{2,1,0:T(2,128)} %bitcast.19, ...), custom_call_target="tpu_custom_call" | custom-call | tf_op jit(solution)/shard_map/pallas_call | solution.py:553
  13.2 0.9 %shard_map.92 = bf16[64,3136]{1,0:T(8,128)(2,1)} custom-call(bf16[64,3136]{1,0:T(8,128)(2,1)S(1)} %get-tuple-element.8.x_ref, f32[64,3200]{1,0:T(8,128)S(1)} %get-tuple-element.9.total, f32[64,128]{1,0:T(8,128)S(1)} %get-tuple-element.10.sums_ref), custom_call_target="tpu_custom_call" | custom-call | tf_op jit(solution)/shard_map/pallas_call | solution.py:601

commit v6 on v5

--- a/solution.py
+++ b/solution.py
@@ -269,15 +269,21 @@
                 (spots >= first) & (spots <= last), rows, 0.0
             ).astype(jnp.bfloat16)
 
-    def spread(edges, spot=0):
+    def spread(edges, spot=0, windows=(0, 1), cuts=1):
         base = spot * edges
-        low = base * len(GROUPS)
-        cut = low + LOW_GROUPS * edges
-        high = low + len(GROUPS) * edges
-        for window, span in enumerate((slice(low, cut), slice(cut, high))):
-            mult[span] = jnp.dot(
-                entries[span], expand[window], preferred_element_type=jnp.float32
-            )
+        for window in windows:
+            first = LOW_GROUPS * window
+            count = len(GROUPS) - LOW_GROUPS if window else LOW_GROUPS
+            edge = [first + count * step // cuts for step in range(cuts + 1)]
+            for start, end in zip(edge[:-1], edge[1:]):
+                span = slice(
+                    (spot * len(GROUPS) + start) * edges, (spot * len(GROUPS) + end) * edges
+                )
+                mult[span] = jnp.dot(
+                    entries[span], expand[window], preferred_element_type=jnp.float32
+                )
+        if 0 not in windows:
+            return
         for number, entry in enumerate(ALONE):
             value = rot_scr[base : base + edges, entry : entry + 1]
             value = jnp.broadcast_to(value, (edges, LANES))
@@ -299,9 +305,10 @@
             lax.broadcasted_iota(jnp.int32, (BLOCK, nodes), 1).astype(jnp.float32) == sources(block)
         ).astype(jnp.bfloat16)
         place(rot_ref, block * group, BLOCK)
+        spread(BLOCK, windows=(0,), cuts=2)
         if block is first_block:
             early[3].wait()
-        spread(BLOCK)
+        spread(BLOCK, windows=(1,), cuts=2)
         xg[:, 0:flat] = jnp.dot(hot, x_ref[...], preferred_element_type=jnp.float32)
         sums = [None] * FRAME
         for slot, tile, number, which in PARTS:

time: 14.3 us -> 14.3 us (level)
  no operation moved by 1% of the time
where the time goes in v6:
time: 14.3 us; the launch traced here: 14.1 us
  Pallas kernels  14.1 us (99%)
    pallas_call x1, Pallas kernels, shards(): pl.pallas_call(functools.partial(kernel, peers, slots), out_shape=(jax.Sh...  13.2 us
    pallas_call x1, Pallas kernels, shards(): pl.pallas_call(functools.partial(finish, chunks), out_shape=jax.ShapeDtyp...  0.89 us

profile of v6, /device:TPU:0, one launch (start us, length us, event | category | flops | bytes accessed | tf_op | source)
XLA Modules:
  0.0 14.1 jit_solution(6211205952969515763)
XLA Ops:
  0.0 13.2 %shard_map.91 = (bf16[64,3136]{1,0:T(8,128)(2,1)S(1)}, f32[64,3200]{1,0:T(8,128)S(1)}, f32[64,128]{1,0:T(8,128)S(1)}) custom-call(bf16[64,3136]{1,0:T(8,128)(2,1)} %bitcast.16, bf16[16,2,235]{2,1,0:T(2,128)(2,1)} %bitcast.17, s32[1,2,16]{2,1,0:T(2,128)} %bitcast.18, s32[1,1,16]{2,1,0:T(1,128)} %bitcast.20, s32[1,2,16]{2,1,0:T(2,128)} %bitcast.19, ...), custom_call_target="tpu_custom_call" | custom-call | tf_op jit(solution)/shard_map/pallas_call | solution.py:560
  13.2 0.9 %shard_map.92 = bf16[64,3136]{1,0:T(8,128)(2,1)} custom-call(bf16[64,3136]{1,0:T(8,128)(2,1)S(1)} %get-tuple-element.8.x_ref, f32[64,3200]{1,0:T(8,128)S(1)} %get-tuple-element.9.total, f32[64,128]{1,0:T(8,128)S(1)} %get-tuple-element.10.sums_ref), custom_call_target="tpu_custom_call" | custom-call | tf_op jit(solution)/shard_map/pallas_call | solution.py:608
